TPU v7x, 32 devices: a whole 2x2x4 slice. The times are simulated.
32 devices in a mesh: dp: 8 (over z, y), mp: 4 (over x, core).
Axes of the slice: x: 2, y: 2, z: 4, core: 2. Of those that a mesh axis runs over, the one named last changes fastest.
Arguments:
- tokens: bfloat16 [8, 1024, 1280], P('dp', 'mp'), may hold values from -6 to 6
- sizes: float32 [8, 1024], P('dp'), may hold values from 1 to 8
- ln1_gain: float32 [1280], replicated, may hold values from 0.25 to 1.75
- qkv_weight: bfloat16 [3, 1280, 1280], P(None, 'dp', 'mp'), may hold values from -0.15625 to 0.15625
- proj_weight: bfloat16 [1280, 1280], P('mp', 'dp'), may hold values from -0.15625 to 0.15625
- ln2_gain: float32 [1280], replicated, may hold values from 0.25 to 1.75
- fc1_weight: bfloat16 [1280, 5120], P('dp', 'mp'), may hold values from -0.15625 to 0.15625
- fc1_bias: float32 [5120], P('mp'), may hold values from -3 to 3
- fc2_weight: bfloat16 [5120, 1280], P('mp', 'dp'), may hold values from -0.078125 to 0.078125
- pair_source: int32 [8, 16], P('dp'), may hold values from 0 to 1022, as said below
- pair_target: int32 [8, 16], P('dp'), may hold values from 1 to 1023, as said below
- kept_order: int32 [8, 1008], P('dp'), may hold values from 0 to 1023, as said below
Outputs:
- merged_out: bfloat16 [8, 1008, 1280], P('dp', 'mp')
Inputs may be any that keep to these rules, and one draw needn't show every extreme that they name: `pair_source`: in each image the 16 entries are distinct even token indices. `pair_target`: odd token indices; several sources may join the same target. `kept_order`: in each image every token index that is not in pair_source appears exactly once.
All inputs are finite; a program needn't handle non-finite values.
Results may differ from a plain program's by a relative error of at most 0.017.
Values may be sent and summed in bfloat16 or wider, within the bound.
A program may use at most 64 MiB of HBM per device.

v0:
```python
import math

import jax
import jax.numpy as jnp
from jax import lax
from jax.sharding import PartitionSpec as P

D = 1280
HEADS = 16


def layer_norm(values, gain):
    center = values - jnp.mean(values, axis=-1, keepdims=True)
    spread = jnp.mean(center * center, axis=-1, keepdims=True)
    return center * lax.rsqrt(spread + 1e-06) * gain


def merge_rows(total, order_rows, source_ids, target_ids):
    kept_rows = jnp.take_along_axis(total, order_rows[:, :, None], axis=1)
    source_rows = jnp.take_along_axis(total, source_ids[:, :, None], axis=1)
    joins = (order_rows[:, :, None] == target_ids[:, None, :]).astype(jnp.float32)
    return kept_rows + jnp.einsum(
        "icr,ird->icd", joins, source_rows, precision=lax.Precision.HIGHEST
    )


def shards(
    tokens,
    sizes,
    ln1_gain,
    qkv_weight,
    proj_weight,
    ln2_gain,
    fc1_weight,
    fc1_bias,
    fc2_weight,
    pair_source,
    pair_target,
    kept_order,
):
    images, own_tokens, width = tokens.shape
    length = sizes.shape[1]
    kept_total = kept_order.shape[1]
    devices_mp = lax.axis_size("mp")
    own_start = lax.axis_index("mp") * own_tokens
    head_size = D // HEADS
    base = tokens.astype(jnp.float32)
    normed = layer_norm(base, ln1_gain).astype(jnp.bfloat16)
    whole = lax.all_gather(normed, "mp", axis=1, tiled=True)
    local_width = qkv_weight.shape[2]
    columns = whole
    projected = jnp.einsum(
        "ind,cdf->cinf",
        columns,
        lax.all_gather(qkv_weight, "dp", axis=1, tiled=True),
        preferred_element_type=jnp.float32,
    ).astype(jnp.bfloat16)
    local_heads = local_width // head_size
    shaped = projected.reshape(3, images, length, local_heads, head_size)
    queries = shaped[0]
    keys_all = shaped[1]
    values_all = shaped[2]
    size_bias = jnp.log(sizes)[:, None, None, :]
    block = min(512, length)
    outputs = []
    for begin in range(0, length, block):
        scores = (
            jnp.einsum(
                "iqhe,ikhe->ihqk",
                queries[:, begin : begin + block],
                keys_all,
                preferred_element_type=jnp.float32,
            )
            / math.sqrt(head_size)
            + size_bias
        )
        weights = jax.nn.softmax(scores, axis=-1).astype(jnp.bfloat16)
        attended_block = jnp.einsum(
            "ihqk,ikhe->iqhe", weights, values_all, preferred_element_type=jnp.float32
        )
        outputs.append(attended_block.astype(jnp.bfloat16).reshape(images, block, local_width))
    attended = jnp.concatenate(outputs, axis=1)
    branch = jnp.einsum(
        "ind,de->ine",
        attended,
        lax.all_gather(proj_weight, "dp", axis=1, tiled=True),
        preferred_element_type=jnp.float32,
    )
    weighted = sizes[:, :, None] * branch
    own_sizes = lax.dynamic_slice_in_dim(sizes, own_start, own_tokens, 1)
    own_weighted = own_sizes[:, :, None] * base
    local_total = lax.dynamic_update_slice_in_dim(
        weighted,
        lax.dynamic_slice_in_dim(weighted, own_start, own_tokens, 1) + own_weighted,
        own_start,
        1,
    )
    merged_count = kept_total // devices_mp
    own_order = lax.dynamic_slice_in_dim(
        kept_order, lax.axis_index("mp") * merged_count, merged_count, 1
    )
    scattered = lax.psum_scatter(
        jnp.transpose(
            merge_rows(local_total, kept_order, pair_source, pair_target), (1, 0, 2)
        ).astype(jnp.bfloat16),
        "mp",
        scatter_dimension=0,
        tiled=True,
    ).astype(jnp.float32)
    numerator = jnp.transpose(scattered, (1, 0, 2))
    merged_size = merge_rows(sizes[:, :, None], own_order, pair_source, pair_target)
    merged = numerator / merged_size
    normed_two = layer_norm(merged, ln2_gain).astype(jnp.bfloat16)
    gathered = lax.all_gather(normed_two, "mp", axis=1, tiled=True)
    columns = gathered
    hidden_sum = jnp.einsum(
        "imd,df->imf",
        columns,
        lax.all_gather(fc1_weight, "dp", axis=0, tiled=True),
        preferred_element_type=jnp.float32,
    )
    hidden = jax.nn.gelu(hidden_sum + fc1_bias).astype(jnp.bfloat16)
    partial_out = jnp.einsum(
        "imf,fd->imd",
        hidden,
        lax.all_gather(fc2_weight, "dp", axis=1, tiled=True),
        preferred_element_type=jnp.float32,
    )
    mlp_part = lax.psum_scatter(
        partial_out.astype(jnp.bfloat16), "mp", scatter_dimension=1, tiled=True
    ).astype(jnp.float32)
    return (merged + mlp_part).astype(jnp.bfloat16)


def solution(mesh):
    return jax.shard_map(
        shards,
        mesh=mesh,
        in_specs=(
            P("dp", "mp", None),
            P("dp", None),
            P(),
            P(None, "dp", "mp"),
            P("mp", "dp"),
            P(),
            P("dp", "mp"),
            P("mp"),
            P("mp", "dp"),
            P("dp", None),
            P("dp", None),
            P("dp", None),
        ),
        out_specs=P("dp", "mp", None),
        check_vma=False,
    )
```

profile of v0, /device:TPU:1, one launch (start us, length us, event | category | flops | bytes accessed | tf_op | source)
XLA Modules:
  0.0 317.7 jit_solution(4380768634615341311)
XLA Ops:
  6.6 1.3 convert_reduce_fusion
  7.9 1.4 fusion.30
  9.3 2.2 fusion.32
  13.8 28.3 %all_gather.20 = bf16[320,1280]{0,1:T(8,128)(2,1)S(1)} all-gather(bf16[320,160]{0,1:T(8,128)(2,1)S(1)} %copy-done.2), channel_id=1, replica_groups=mesh['dp'=8,'mp'=4] {'dp'}, dimensions={1}, use_global_device_ids=true | all-gather | bytes 921600 | tf_op jit(solution)/shard_map/all_gather | solution.py:86
  42.8 1.4 gather_fusion.2
  44.4 53.4 %all-gather.8.cloned.1.call-done = bf16[3,1280,320]{2,1,0:T(8,128)(2,1)} async-done(((bf16[3,160,320]{2,1,0:T(8,128)(2,1)}), bf16[3,1280,320]{2,1,0:T(8,128)(2,1)}) %all-gather.8.cloned.1.call-update) | async-done | bytes 2457616 | tf_op jit(solution)/shard_map/all_gather | solution.py:55
  97.8 5.4 %convert_bitcast_fusion = bf16[3,1,1024,320]{2,3,0,1:T(8,128)(2,1)S(1)} fusion(bf16[3,1280,320]{2,1,0:T(8,128)(2,1)} %all-gather.8.cloned.1.call-done, bf16[1,1024,1280]{2,1,0:T(8,128)(2,1)} %all-gather.6.cloned.1.call-done), kind=kOutput, calls=%fused_computation.38 | convolution fusion | flops 2517565440 | bytes 7045120 | tf_op jit(solution)/shard_map/ind,cdf->cinf/dot_general | solution.py:52
  103.3 4.9 %fusion.80 = (f32[4,512]{1,0:T(4,128)S(1)}, f32[4,512,1024]{2,1,0:T(8,128)}) fusion(f32[1024]{0:T(1024)S(1)} %bitcast.179, bf16[1024,4,80]{0,2,1:T(8,128)(2,1)S(1)} %bitcast.170, bf16[1,1024,4,80]{1,3,2,0:T(8,128)(2,1)S(1)} %bitcast.168), kind=kOutput, calls=%fused_computation.120 | convolution fusion | flops 343933952 | bytes 9383936 | tf_op jit(solution)/shard_map/sub | solution.py:77
  108.2 4.9 %fusion.79 = (f32[4,512]{1,0:T(4,128)S(1)}, f32[4,512,1024]{2,1,0:T(8,128)}) fusion(f32[1024]{0:T(1024)S(1)} %bitcast.180, bf16[1024,4,80]{0,2,1:T(8,128)(2,1)S(1)} %bitcast.171, bf16[1,1024,4,80]{1,3,2,0:T(8,128)(2,1)S(1)} %bitcast.169), kind=kOutput, calls=%fused_computation.119 | convolution fusion | flops 343933952 | bytes 9383936 | tf_op jit(solution)/shard_map/sub | solution.py:77
  113.0 5.1 %fusion.37 = bf16[4,80,512]{2,1,0:T(8,128)(2,1)S(1)} fusion(bf16[1024,4,80]{0,2,1:T(8,128)(2,1)S(1)} %bitcast.166, f32[4,512,1024]{2,1,0:T(8,128)} %get-tuple-element.13, f32[4,512]{1,0:T(4,128)S(1)} %get-tuple-element.12), kind=kOutput, calls=%fused_computation.55 | convolution fusion | flops 339902464 | bytes 9379840 | tf_op jit(solution)/shard_map/ihqk,ikhe->iqhe/dot_general | solution.py:78
  118.9 1.7 fusion.36
  120.6 4.0 %convolution_multiply_fusion = f32[1024,1280]{1,0:T(8,128)} fusion(bf16[320,1280]{0,1:T(8,128)(2,1)S(1)} %all_gather.20, f32[1024]{0:T(1024)S(1)} %bitcast.165, bf16[1,512,320]{1,2,0:T(8,128)(2,1)S(1)} %bitcast.173, bf16[1,512,320]{1,2,0:T(8,128)(2,1)S(1)} %bitcast.172), kind=kOutput, calls=%fused_computation.24 | convolution fusion | flops 841482240 | bytes 6721536 | tf_op jit(solution)/shard_map/ind,de->ine/dot_general | solution.py:83
  124.6 1.4 constant_dynamic-slice_fusion.2
  127.3 3.1 gather_fusion.1
  130.5 9.7 %gather_fusion = f32[1008,1280]{1,0:T(8,128)} fusion(f32[1024,1280]{1,0:T(8,128)} %fusion.35, s32[1024]{0:T(1024)S(1)} %pad_clamp_fusion.2), kind=kCustom, calls=%fused_computation | custom fusion | bytes 10325952 | tf_op jit(solution)/shard_map/jit(take_along_axis)/gather | solution.py:19
  140.1 5.1 %fusion.21 = bf16[1008,1,1280]{2,0,1:T(8,128)(2,1)S(1)} fusion(f32[1008,1280]{1,0:T(8,128)} %gather_fusion, pred[1008]{0:T(1024)(128)(4,1)S(1)} %compare_and_fusion, f32[16,1280]{1,0:T(8,128)S(1)} %gather_fusion.1, pred[16]{0:T(512)(128)(4,1)S(1)} %compare_and_fusion.1, s32[1008]{0:T(1024)S(1)} %bitcast.175, s32[16]{0:T(128)S(1)} %bitcast.185), kind=kOutput, calls=%fused_computation.33 | convolution fusion | flops 251633408 | bytes 7828480 | tf_op jit(solution)/shard_map/icr,ird->icd/dot_general | solution.py:22
  145.2 27.6 %fusion = bf16[256,1280]{1,0:T(8,128)(2,1)S(1)} fusion(bf16[1008,1,1280]{2,0,1:T(8,128)(2,1)S(1)} %fusion.21), kind=kCustom, calls=%all-reduce-scatter | all-reduce-scatter fusion | flops 1310721 | bytes 3236352
  172.8 4.4 %collective-permute-start = (bf16[12,1280]{1,0:T(8,128)(2,1)S(1)}, bf16[12,1280]{1,0:T(8,128)(2,1)S(1)}, u32[]{:S(2)}, u32[]{:S(2)}) collective-permute-start(bf16[12,1280]{1,0:T(8,128)(2,1)S(1)} %slice.36), channel_id=1, source_target_pairs={{0,1},{1,2},{2,3},{4,5},{5,6},{6,7},{8,9},{9,10},{10,11},{12,13},{... | collective-permute-start | bytes 92168
  180.9 2.1 copy.14
  183.1 39.2 %all-gather.14.cloned.1.call-done = bf16[1280,1280]{0,1:T(8,128)(2,1)} async-done(((bf16[1280,160]{0,1:T(8,128)(2,1)}), bf16[1280,1280]{0,1:T(8,128)(2,1)}) %all-gather.14.cloned.1.call-update) | async-done | bytes 3276816 | tf_op jit(solution)/shard_map/all_gather | solution.py:126
  222.2 42.2 %all-gather.10.cloned.1.call-done = bf16[1,1008,1280]{2,0,1:T(2,128)(2,1)} async-done(((bf16[1,252,1280]{2,0,1:T(2,128)(2,1)}), bf16[1,1008,1280]{2,0,1:T(2,128)(2,1)}) %all-gather.10.cloned.1.call-update) | async-done | bytes 2580496 | tf_op jit(solution)/shard_map/all_gather | solution.py:114
  264.5 12.8 %fusion.20 = bf16[1,1008,1280]{2,1,0:T(8,128)(2,1)} fusion(bf16[1280,1280]{0,1:T(8,128)(2,1)} %all-gather.14.cloned.1.call-done, bf16[1280,1280]{1,0:T(8,128)(2,1)} %all-gather.12.cloned.1.call-done, bf16[1,1008,1280]{2,0,1:T(2,128)(2,1)} %all-gather.10.cloned.1.call-done, f32[1280]{0:T(1024)S(1)} %copy-done.7), kind=kOutput, calls=%fused_computation.32 | convolution fusion | flops 6620221440 | bytes 11719680 | tf_op jit(solution)/shard_map/imf,fd->imd/dot_general | solution.py:123
  277.3 26.0 %fusion.1 = bf16[256,1280]{1,0:T(8,128)(2,1)S(1)} fusion(bf16[1,1008,1280]{2,1,0:T(8,128)(2,1)} %fusion.20), kind=kCustom, calls=%all-reduce-scatter.1 | all-reduce-scatter fusion | flops 1310721 | bytes 3236352
  303.4 4.4 %collective-permute-start.1 = (bf16[12,1280]{1,0:T(8,128)(2,1)S(1)}, bf16[12,1280]{1,0:T(8,128)(2,1)S(1)}, u32[]{:S(2)}, u32[]{:S(2)}) collective-permute-start(bf16[12,1280]{1,0:T(8,128)(2,1)S(1)} %slice.37), channel_id=1, source_target_pairs={{0,1},{1,2},{2,3},{4,5},{5,6},{6,7},{8,9},{9,10},{10,11},{12,13},{... | collective-permute-start | bytes 92168
  (62 shorter events, 11.8 us)
Async XLA Ops:
  6.5 7.1 %copy-start.8 = (s32[1,16]{1,0:T(1,128)S(1)}, s32[1,16]{1,0:T(1,128)}, u32[]{:S(2)}) copy-start(s32[1,16]{1,0:T(1,128)} %param.21) | copy-start | bytes 196
  6.5 7.2 %copy-start = (f32[1,1024]{1,0:T(1,128)S(1)}, f32[1,1024]{1,0:T(1,128)}, u32[]{:S(2)}) copy-start(f32[1,1024]{1,0:T(1,128)} %param.13) | copy-start | bytes 12292
  6.5 7.2 %copy-start.2 = (bf16[320,160]{0,1:T(8,128)(2,1)S(1)}, bf16[320,160]{0,1:T(8,128)(2,1)}, u32[]{:S(2)}) copy-start(bf16[320,160]{0,1:T(8,128)(2,1)} %param.16) | copy-start | bytes 307204
  6.5 35.5 %copy-start.3 = (s32[1,1008]{1,0:T(1,128)S(1)}, s32[1,1008]{1,0:T(1,128)}, u32[]{:S(2)}) copy-start(s32[1,1008]{1,0:T(1,128)} %param.23) | copy-start | bytes 12100
  6.5 37.8 %all-gather.6.cloned.1.call-start = ((), (), s32[]{:S(2)}) async-start(), calls=%async_computation | async-start | bytes 3276800 | tf_op jit(solution)/shard_map/all_gather | solution.py:49
  7.9 36.3 %copy-start.5 = (s32[1,16]{1,0:T(1,128)S(1)}, s32[1,16]{1,0:T(1,128)}, u32[]{:S(2)}) copy-start(s32[1,16]{1,0:T(1,128)} %param.22) | copy-start | bytes 196
  11.6 86.2 %all-gather.8.cloned.1.call-start = ((), (), s32[]{:S(2)}) async-start(), calls=%async_computation.1 | async-start | bytes 3317760 | tf_op jit(solution)/shard_map/all_gather | solution.py:55
  12.3 170.7 %all-gather.12.cloned.1.call-start = ((), (), s32[]{:S(2)}) async-start(), calls=%async_computation.3 | async-start | bytes 3686400 | tf_op jit(solution)/shard_map/all_gather | solution.py:119
  13.0 209.2 %all-gather.14.cloned.1.call-start = ((), (), s32[]{:S(2)}) async-start(), calls=%async_computation.4 | async-start | bytes 3686400 | tf_op jit(solution)/shard_map/all_gather | solution.py:126
  13.6 250.8 %all-gather.10.cloned.1.call-start = ((), (), s32[]{:S(2)}) async-start(), calls=%async_computation.2 | async-start | bytes 6451200 | tf_op jit(solution)/shard_map/all_gather | solution.py:114
  113.0 5.9 %copy-start.9 = (f32[4,512,1024]{2,1,0:T(8,128)S(1)}, f32[4,512,1024]{2,1,0:T(8,128)}, u32[]{:S(2)}) copy-start(f32[4,512,1024]{2,1,0:T(8,128)} %get-tuple-element.11) | copy-start | bytes 25165828
  120.6 5.4 %copy-start.1 = (bf16[1,256,1280]{2,1,0:T(8,128)(2,1)S(1)}, bf16[1,256,1280]{2,1,0:T(8,128)(2,1)}, u32[]{:S(2)}) copy-start(bf16[1,256,1280]{2,1,0:T(8,128)(2,1)} %param.12) | copy-start | bytes 1966084
  145.2 32.0 %copy-start.6 = (u32[32]{0:T(128)S(1)}, u32[32]{0:T(128)}, u32[]{:S(2)}) copy-start(u32[32]{0:T(128)} %constant.99) | copy-start | bytes 388
  145.2 35.3 %copy-start.4 = (f32[1280]{0:T(1024)S(1)}, f32[1280]{0:T(1024)}, u32[]{:S(2)}) copy-start(f32[1280]{0:T(1024)} %param.17) | copy-start | bytes 15364
  172.8 5.7 %collective-permute-start = (bf16[12,1280]{1,0:T(8,128)(2,1)S(1)}, bf16[12,1280]{1,0:T(8,128)(2,1)S(1)}, u32[]{:S(2)}, u32[]{:S(2)}) collective-permute-start(bf16[12,1280]{1,0:T(8,128)(2,1)S(1)} %slice.36), channel_id=1, source_target_pairs={{0,1},{1,2},{2,3},{4,5},{5,6},{6,7},{8,9},{9,10},{10,11},{12,13},{... | collective-permute-start | bytes 92168
  179.6 84.9 %copy-start.7 = (f32[1280]{0:T(1024)S(1)}, f32[1280]{0:T(1024)}, u32[]{:S(2)}) copy-start(f32[1280]{0:T(1024)} %param.19) | copy-start | bytes 15364
  303.4 5.5 %collective-permute-start.1 = (bf16[12,1280]{1,0:T(8,128)(2,1)S(1)}, bf16[12,1280]{1,0:T(8,128)(2,1)S(1)}, u32[]{:S(2)}, u32[]{:S(2)}) collective-permute-start(bf16[12,1280]{1,0:T(8,128)(2,1)S(1)} %slice.37), channel_id=1, source_target_pairs={{0,1},{1,2},{2,3},{4,5},{5,6},{6,7},{8,9},{9,10},{10,11},{12,13},{... | collective-permute-start | bytes 92168
Sparse Core Ops, SparseCore 0:
  11.7 27.9 all-gather.5
  41.9 55.8 all-gather.7
  100.0 59.9 all-gather.11
  162.0 60.1 all-gather.13
  223.6 40.7 all-gather.9
where the time goes:
time: 318 us
  waiting for transfers between devices  138 us (43%)
  blocking collectives  81.9 us (26%)
  matrix products  44 us (14%)
  local copies, waits for them, and re-layouts  22 us (7%)
  between operations  14.1 us (4%)
  starting transfers between devices  8.96 us (3%)
  other arithmetic  8.93 us (3%)
    unnamed x2, blocking collectives  53.6 us
    all_gather x1, waiting for transfers between devices, shards(): lax.all_gather(qkv_weight, 'dp', axis=1, tiled=True)  53.4 us
    all_gather x1, waiting for transfers between devices, shards(): gathered = lax.all_gather(normed_two, 'mp', axis=1, tiled=True)  42.2 us
    all_gather x1, waiting for transfers between devices, shards(): lax.all_gather(fc2_weight, 'dp', axis=1, tiled=True)  39.2 us
    all_gather x1, blocking collectives, shards(): lax.all_gather(proj_weight, 'dp', axis=1, tiled=True)  28.3 us
    dot_general x1, matrix products, shards(): jnp.einsum('imf,fd->imd', hidden, lax.all_gather(fc2_weight, 'dp', axis=1...  12.8 us
    gather x2, local copies, waits for them, and re-layouts, merge_rows(): kept_rows = jnp.take_along_axis(total, order_rows[:, :, None], axis=1)  11 us
    sub x2, matrix products, shards(): weights = jax.nn.softmax(scores, axis=-1).astype(jnp.bfloat16)  9.7 us
  transfers between devices with their start and end apart: 7, of which 4 were waited for; matrix products, arithmetic and copies ran while one was open for 26% of the time, Pallas kernels for 0%

commit v1 on v0

v1 whole, which is shorter than its diff:
```python
import functools
import math

import jax
import jax.numpy as jnp
from jax import lax
from jax.experimental import pallas as pl
from jax.experimental.pallas import tpu as pltpu
from jax.sharding import PartitionSpec as P

HEADS = 16


def layer_norm(values, gain):
    center = values - jnp.mean(values, axis=-1, keepdims=True)
    spread = jnp.mean(center * center, axis=-1, keepdims=True)
    return center * lax.rsqrt(spread + 1e-06) * gain


def powers(count):
    bits = []
    bit = 1
    while bit < count:
        bits.append(bit)
        bit *= 2
    return bits


def toggled(index, mask):
    for bit in powers(mask + 1):
        if mask & bit:
            index = index + bit * (1 - 2 * lax.rem(lax.div(index, bit), 2))
    return index


def greet(peers):
    barrier = pltpu.get_barrier_semaphore()
    for axis, peer in peers:
        pl.semaphore_signal(
            barrier, inc=1, device_id={axis: peer}, device_id_type=pl.DeviceIdType.MESH
        )
    pl.semaphore_wait(barrier, len(peers))


class Copies:
    def __init__(self, send, recv):
        self.send, self.recv, self.made = send, recv, []

    def start(self, source, target, axis, peer):
        number = len(self.made)
        copy = pltpu.make_async_remote_copy(
            src_ref=source,
            dst_ref=target,
            send_sem=self.send.at[number],
            recv_sem=self.recv.at[number],
            device_id={axis: peer},
            device_id_type=pl.DeviceIdType.MESH,
        )
        copy.start()
        self.made.append(copy)
        return copy


def rows_of(out, owner, rows):
    span = pl.ds(pl.multiple_of(owner * rows, 16), rows)
    if len(out.shape) == 3:
        return out.at[:, span, :]
    return out.at[span, :]


class Waits:
    def __init__(self):
        self.seen = set()

    def ready(self, copy):
        if id(copy) not in self.seen:
            copy.wait_recv()
            self.seen.add(id(copy))


def dp_peers(dp):
    me = lax.axis_index("dp")
    return me, toggled(me, 1), lax.rem(me + 2, dp), lax.rem(me + dp - 2, dp)


def start_dp(own, out, copies, dp):
    me, pair, after, before = dp_peers(dp)
    here = rows_of(out, me, own.shape[-2])
    return [copies.start(own, here, "dp", peer) for peer in (pair, after, before)]


def relay_dp(own, out, copies, waits, state, dp, step):
    me, pair, after, before = dp_peers(dp)
    ring = dp // 2
    rows = own.shape[-2]
    other, forward, backward = state
    block = rows_of(out, lax.rem(me - 2 * step + 2 * dp, dp), rows)
    waits.ready(forward)
    if step < ring // 2:
        state[1] = copies.start(block, block, "dp", after)
    copies.start(block, block, "dp", pair)
    if step < ring - step:
        block = rows_of(out, toggled(lax.rem(me + 2 * (step - 1), dp), 1), rows)
        waits.ready(other)
        state[0] = copies.start(block, block, "dp", before)
        if step + 1 < ring - step - 1:
            block = rows_of(out, lax.rem(me + 2 * step, dp), rows)
            waits.ready(backward)
            state[2] = copies.start(block, block, "dp", before)


def gather_kernel(dp, mp, *refs):
    own, out = refs[:2], refs[2:4]
    send, recv, local = refs[4:]
    at = lax.axis_index("mp")
    me, pair, after, before = dp_peers(dp)
    greet(
        [("mp", toggled(at, bit)) for bit in powers(mp)]
        + [("dp", pair), ("dp", after), ("dp", before)]
    )
    copies, waits = Copies(send, recv), Waits()
    heads = start_dp(own[1], out[1], copies, dp)
    mine = rows_of(out[0], at, own[0].shape[0])
    bits = list(reversed(powers(mp)))
    here = {bit: copies.start(own[0], mine, "mp", toggled(at, bit)) for bit in bits}
    stays = []
    for number, owner in ((0, at), (1, me)):
        keep = pltpu.make_async_copy(
            own[number], rows_of(out[number], owner, own[number].shape[-2]), local.at[number]
        )
        keep.start()
        stays.append(keep)
    relay_dp(own[1], out[1], copies, waits, heads, dp, 1)
    held = [0]
    for bit in bits:
        for k in list(held):
            if k:
                waits.ready(here[k])
                block = rows_of(out[0], toggled(at, k), own[0].shape[0])
                here[k ^ bit] = copies.start(block, block, "mp", toggled(at, bit))
            held.append(k ^ bit)
    for step in range(2, dp // 4 + 1):
        relay_dp(own[1], out[1], copies, waits, heads, dp, step)
    for copy in copies.made:
        waits.ready(copy)
        copy.wait_send()
    for keep in stays:
        keep.wait()


def gather_all(normed, heads):
    dp, mp = lax.axis_size("dp"), lax.axis_size("mp")
    total = (mp - 1) + (dp - 1)
    shapes = [
        (mp * normed.shape[0], normed.shape[1]),
        (dp * heads.shape[0], heads.shape[1]),
    ]
    return pl.pallas_call(
        functools.partial(gather_kernel, dp, mp),
        out_shape=[jax.ShapeDtypeStruct(shape, jnp.bfloat16) for shape in shapes],
        in_specs=[pl.BlockSpec(memory_space=pltpu.VMEM)] * 2,
        out_specs=[pl.BlockSpec(memory_space=pl.ANY)] * 2,
        scratch_shapes=[
            pltpu.SemaphoreType.DMA((total,)),
            pltpu.SemaphoreType.DMA((total,)),
            pltpu.SemaphoreType.DMA((2,)),
        ],
        compiler_params=pltpu.CompilerParams(collective_id=0, has_side_effects=True),
        cost_estimate=pl.CostEstimate(
            flops=10**10, bytes_accessed=10**8, transcendentals=0
        ),
        name="gather_all",
    )(normed, heads)


def reduce_kernel(dp, mp, last, *refs):
    if last:
        parts, extra, out, held, landing, send, recv = refs
    else:
        parts, extra, own, out, whole, weight, held, landing, normed, send, recv, local = refs
    at = lax.axis_index("mp")
    peers = [("mp", toggled(at, bit)) for bit in powers(mp)]
    if not last:
        peers += [("dp", peer) for peer in dp_peers(dp)[1:]]
    greet(peers)
    copies, waits = Copies(send, recv), Waits()
    slots = 0
    stored = {k: None for k in range(mp)}
    if not last:
        state = start_dp(own, weight, copies, dp)
        rest = pltpu.make_async_copy(
            own, rows_of(weight, lax.axis_index("dp"), own.shape[0]), local.at[1]
        )
        rest.start()

    def source(k):
        return parts.at[toggled(at, k)] if stored[k] is None else held.at[k]

    for bit in powers(mp):
        moving = [k for k in reversed(range(mp)) if k in stored and k & bit]
        flights = []
        for k in moving:
            flights.append(
                (k, slots, copies.start(source(k), landing.at[slots], "mp", toggled(at, bit)))
            )
            slots += 1
        for k, slot, copy in flights:
            waits.ready(copy)
            kept = k ^ bit
            total = source(kept)[...].astype(jnp.float32) + landing[slot].astype(jnp.float32)
            if 2 * bit < mp:
                held[kept] = total.astype(jnp.bfloat16)
                stored[kept] = True
            del stored[k]
        if not last and bit == 1:
            relay_dp(own, weight, copies, waits, state, dp, 1)
    if last:
        out[...] = (extra[...] + total).astype(out.dtype)
    else:
        out[...] = total
        normed[...] = layer_norm(total, extra[...]).astype(jnp.bfloat16)
        keep = pltpu.make_async_copy(normed, whole.at[at], local.at[0])
        keep.start()
        bits = list(reversed(powers(mp)))
        here = {
            bit: copies.start(normed, whole.at[at], "mp", toggled(at, bit)) for bit in bits
        }
        for step in range(2, dp // 4 + 1):
            relay_dp(own, weight, copies, waits, state, dp, step)
        near = [0]
        for bit in bits:
            for k in list(near):
                if k:
                    waits.ready(here[k])
                    block = whole.at[toggled(at, k)]
                    here[k ^ bit] = copies.start(block, block, "mp", toggled(at, bit))
                near.append(k ^ bit)
        keep.wait()
        rest.wait()
    for copy in copies.made:
        waits.ready(copy)
        copy.wait_send()


def reduce_parts(parts, extra, own=None):
    mp, rows, width = parts.shape
    dp = lax.axis_size("dp")
    last = own is None
    operands = [parts, extra] if last else [parts, extra, own]
    vmem = pl.BlockSpec(memory_space=pltpu.VMEM)
    out_shape = [
        jax.ShapeDtypeStruct((rows, width), jnp.bfloat16 if last else jnp.float32)
    ]
    out_specs = [vmem]
    scratch = [
        pltpu.VMEM((mp, rows, width), jnp.bfloat16),
        pltpu.VMEM((mp - 1, rows, width), jnp.bfloat16),
    ]
    total = mp - 1
    if not last:
        out_shape.append(jax.ShapeDtypeStruct((mp, rows, width), jnp.bfloat16))
        out_shape.append(jax.ShapeDtypeStruct((dp * own.shape[0], own.shape[1]), jnp.bfloat16))
        out_specs += [pl.BlockSpec(memory_space=pl.ANY)] * 2
        scratch.append(pltpu.VMEM((rows, width), jnp.bfloat16))
        total = 2 * total + dp - 1
    scratch += [pltpu.SemaphoreType.DMA((total,)), pltpu.SemaphoreType.DMA((total,))]
    if not last:
        scratch.append(pltpu.SemaphoreType.DMA((2,)))
    return pl.pallas_call(
        functools.partial(reduce_kernel, dp, mp, last),
        out_shape=out_shape,
        in_specs=[vmem] * len(operands),
        out_specs=out_specs,
        scratch_shapes=scratch,
        compiler_params=pltpu.CompilerParams(
            collective_id=2 if last else 1, has_side_effects=True
        ),
        cost_estimate=pl.CostEstimate(
            flops=10**10, bytes_accessed=10**8, transcendentals=0
        ),
        name="reduce_last" if last else "reduce_norm_gather",
    )(*operands)


def shards(
    tokens,
    sizes,
    ln1_gain,
    qkv_weight,
    proj_weight,
    ln2_gain,
    fc1_weight,
    fc1_bias,
    fc2_weight,
    pair_source,
    pair_target,
    kept_order,
):
    images, own_tokens, width = tokens.shape
    length = sizes.shape[1]
    kept_total = kept_order.shape[1]
    count = lax.axis_size("mp")
    me = lax.axis_index("mp")
    kept_own = kept_total // count
    padded = -(-kept_own // 16) * 16
    head_size = width // HEADS
    local_width = qkv_weight.shape[2]
    local_heads = local_width // head_size

    base = tokens.astype(jnp.float32)
    normed = layer_norm(base, ln1_gain).astype(jnp.bfloat16)
    whole, heads_whole = gather_all(
        normed.reshape(own_tokens, width),
        jnp.concatenate(
            [qkv_weight[0], qkv_weight[1], qkv_weight[2], proj_weight.T], axis=1
        ),
    )
    whole = whole[None]
    whole, heads_whole, late = lax.optimization_barrier((whole, heads_whole, fc1_weight))
    fc1 = lax.all_gather(late, "dp", axis=0, tiled=True)

    positions = jnp.arange(length, dtype=jnp.int32)
    order = jnp.pad(
        kept_order.reshape(images, count, kept_own),
        ((0, 0), (0, 0), (0, padded - kept_own)),
        constant_values=-1,
    ).reshape(images, count * padded)
    hits = positions[None, None, :] == pair_source[:, :, None]
    destination = positions[None, :] + jnp.sum(
        jnp.where(hits, pair_target[:, :, None] - positions[None, None, :], 0), axis=1
    )
    joins = order[:, :, None] == destination[:, None, :]
    shares = jnp.where(joins, sizes[:, None, :], 0.0)
    merged_size = jnp.sum(shares, axis=2, keepdims=True)
    shares = (shares / jnp.where(merged_size > 0, merged_size, 1.0)).astype(jnp.bfloat16)
    own_shares = lax.dynamic_slice_in_dim(shares, me * own_tokens, own_tokens, 2)

    projected = jnp.einsum(
        "ind,df->inf", whole, heads_whole[:, : 3 * local_width], preferred_element_type=jnp.float32
    ).astype(jnp.bfloat16)
    shaped = [
        projected[:, :, c * local_width : (c + 1) * local_width].reshape(
            images, length, local_heads, head_size
        )
        for c in range(3)
    ]
    size_bias = jnp.log(sizes)[:, None, None, :]
    block = min(512, length)
    outputs = []
    for begin in range(0, length, block):
        scores = (
            jnp.einsum(
                "iqhe,ikhe->ihqk",
                shaped[0][:, begin : begin + block],
                shaped[1],
                preferred_element_type=jnp.float32,
            )
            / math.sqrt(head_size)
            + size_bias
        )
        weights = jax.nn.softmax(scores, axis=-1).astype(jnp.bfloat16)
        outputs.append(
            jnp.einsum("ihqk,ikhe->iqhe", weights, shaped[2], preferred_element_type=jnp.float32)
            .astype(jnp.bfloat16)
            .reshape(images, block, local_width)
        )
    attended = jnp.concatenate(outputs, axis=1)

    joined = jnp.einsum(
        "ijn,ind->ijd", shares, attended, preferred_element_type=jnp.float32
    ).astype(jnp.bfloat16)

    left, right = lax.optimization_barrier(
        (
            jnp.concatenate([joined, own_shares], axis=2),
            jnp.concatenate([heads_whole[:, 3 * local_width :].T, tokens[0]], axis=0),
        )
    )
    parts = jnp.einsum("ijd,de->ije", left, right, preferred_element_type=jnp.float32)
    parts = parts.astype(jnp.bfloat16).reshape(count, padded, width)
    merged, gathered, fc2 = reduce_parts(parts, ln2_gain.reshape(1, width), fc2_weight.T)
    hidden_sum = jnp.einsum(
        "md,df->mf", gathered.reshape(count * padded, width), fc1,
        preferred_element_type=jnp.float32,
    )
    hidden = jax.nn.gelu(hidden_sum + fc1_bias).astype(jnp.bfloat16)
    partial_out = jnp.einsum("mf,df->md", hidden, fc2, preferred_element_type=jnp.float32)
    partial_out = partial_out.astype(jnp.bfloat16).reshape(count, padded, width)
    out = reduce_parts(partial_out, merged)[0]
    return out[None, :kept_own]


def solution(mesh):
    return jax.shard_map(
        shards,
        mesh=mesh,
        in_specs=(
            P("dp", "mp", None),
            P("dp", None),
            P(),
            P(None, "dp", "mp"),
            P("mp", "dp"),
            P(),
            P("dp", "mp"),
            P("mp"),
            P("mp", "dp"),
            P("dp", None),
            P("dp", None),
            P("dp", None),
        ),
        out_specs=P("dp", "mp", None),
        check_vma=False,
    )
```

time: 318 us -> 202 us (0.64)
  waiting for transfers between devices: 138 us -> 0.04 us
  Pallas kernels: 0 us -> 130 us
  blocking collectives: 81.9 us -> 0 us
  local copies, waits for them, and re-layouts: 22 us -> 8.58 us
  starting transfers between devices: 8.96 us -> 0.01 us
  matrix products: 44 us -> 38.8 us
    all_gather x5 -> x1, waiting for transfers between devices: 135 us -> 0.02 us  [shards(): fc1 = lax.all_gather(late, 'dp', axis=0, tiled=True)]
    pallas_call x0 -> x3, Pallas kernels: none -> 130 us  [the longest x2 87.4 us: reduce_parts(): pl.pallas_call(functools.partial(reduce_kernel, dp, mp, last), out_shape=...]
    unnamed x2 -> x0, blocking collectives: 53.6 us -> none
    all_gather x1 -> x0, blocking collectives: 28.3 us -> none  [shards(): lax.all_gather(proj_weight, 'dp', axis=1, tiled=True)]
    gather x4 -> x0, local copies, waits for them, and re-layouts: 14.8 us -> none  [the longest x2 11 us: merge_rows(): kept_rows = jnp.take_along_axis(total, order_rows[:, :, None], axis=1)]
    unnamed x2 -> x0, starting transfers between devices: 8.77 us -> none
    dot_general x7 -> x6, matrix products: 34.3 us -> 29.1 us  [the longest x1 12.2 us: shards(): jnp.einsum('mf,df->md', hidden, fc2, preferred_element_type=jnp.float32)]
  transfers between devices with their start and end apart: 7 -> 1, of which waited for: 4 -> 0; matrix products, arithmetic and copies ran while one was open for 26% -> 17% of each run, Pallas kernels for 0% -> 31%
where the time goes in v1:
time: 202 us; the launch traced here: 201 us
  Pallas kernels  130 us (64%)
  matrix products  38.8 us (19%)
  between operations  13.6 us (7%)
  other arithmetic  10 us (5%)
  local copies, waits for them, and re-layouts  8.58 us (4%)
    pallas_call x2, Pallas kernels, reduce_parts(): pl.pallas_call(functools.partial(reduce_kernel, dp, mp, last), out_shape=...  87.4 us
    pallas_call x1, Pallas kernels, gather_all(): pl.pallas_call(functools.partial(gather_kernel, dp, mp), out_shape=[jax.S...  42.3 us
    dot_general x1, matrix products, shards(): jnp.einsum('mf,df->md', hidden, fc2, preferred_element_type=jnp.float32)  12.2 us
    sub x2, matrix products, shards(): weights = jax.nn.softmax(scores, axis=-1).astype(jnp.bfloat16)  9.7 us
    dot_general x2, matrix products, shards(): jnp.einsum('ihqk,ikhe->iqhe', weights, shaped[2], preferred_element_type=...  6.76 us
    dot_general x1, matrix products, shards(): jnp.einsum('ind,df->inf', whole, heads_whole[:, :3 * local_width], prefer...  5.29 us
  transfers between devices with their start and end apart: 1, of which 0 were waited for; matrix products, arithmetic and copies ran while one was open for 17% of the time, Pallas kernels for 31%

profile of v1, /device:TPU:1, one launch (start us, length us, event | category | flops | bytes accessed | tf_op | source)
XLA Modules:
  0.0 200.8 jit_solution(8496919089053960590)
XLA Ops:
  6.5 1.1 slice_bitcast_fusion.16
  7.6 1.3 convert_reduce_fusion
  8.9 1.4 fusion.38
  10.3 2.2 %fusion.53.refs_0_ = bf16[256,1280]{1,0:T(8,128)(2,1)} fusion(bf16[1,256,1280]{2,1,0:T(8,128)(2,1)} %param.12, f32[1280]{0:T(1024)} %param.14, f32[256]{0:T(256)S(1)} %add_rsqrt_fusion, f32[256]{0:T(256)S(1)} %broadcast_multiply_fusion), kind=kLoop, calls=%fused_computation.60 | loop fusion | flops 1638400 | bytes 1317888 | tf_op jit(solution)/shard_map/reshape | solution.py:313
  12.5 1.0 concatenate.12.refs_1_
  13.5 42.3 %gather_all.1 = (bf16[1024,1280]{1,0:T(8,128)(2,1)}, bf16[1280,1280]{1,0:T(8,128)(2,1)}) custom-call(bf16[256,1280]{1,0:T(8,128)(2,1)} %fusion.53.refs_0_, bf16[160,1280]{1,0:T(8,128)(2,1)} %concatenate.12.refs_1_), custom_call_target="tpu_custom_call" | custom-call | flops 10000000000 | bytes 100000000 | tf_op jit(solution)/shard_map/gather_all/pallas_call | solution.py:158
  56.1 5.3 %convert_bitcast_fusion = bf16[1,1024,960]{1,2,0:T(8,128)(2,1)S(1)} fusion(bf16[1280,1280]{1,0:T(8,128)(2,1)} %get-tuple-element.18, bf16[1,1024,1280]{2,1,0:T(8,128)(2,1)} %bitcast.112), kind=kOutput, calls=%fused_computation.39 | convolution fusion | flops 2517565440 | bytes 7208960 | tf_op jit(solution)/shard_map/ind,df->inf/dot_general | solution.py:338
  62.1 0.5 broadcast.376
  62.6 0.7 reduce.15
  63.5 2.5 %fusion.51 = (f32[1024]{0:T(1024)S(1)}, f32[1,1024,1024]{1,2,0:T(8,128)}) fusion(f32[1024]{0:T(1024)S(1)} %bitcast.103, s32[1024]{0:T(1024)S(1)} %iota_add_fusion, s32[1024]{0:T(1024)S(1)} %bitcast.105), kind=kLoop, calls=%fused_computation.56 | loop fusion | flops 3144704 | bytes 4210688 | tf_op jit(solution)/shard_map/reduce_sum | solution.py:334
  66.0 4.8 %fusion.68 = (f32[4,512]{1,0:T(4,128)S(1)}, f32[4,512,1024]{2,1,0:T(8,128)}) fusion(f32[1024]{0:T(1024)S(1)} %bitcast.107, bf16[1024,4,80]{0,2,1:T(8,128)(2,1)S(1)} %bitcast.100, bf16[1,1024,4,80]{1,3,2,0:T(8,128)(2,1)S(1)} %bitcast.98), kind=kOutput, calls=%fused_computation.89 | convolution fusion | flops 343933952 | bytes 9383936 | tf_op jit(solution)/shard_map/sub | solution.py:361
  70.8 1.3 fusion.52
  72.1 4.9 %fusion.67 = (f32[4,512]{1,0:T(4,128)S(1)}, f32[4,512,1024]{2,1,0:T(8,128)}) fusion(f32[1024]{0:T(1024)S(1)} %bitcast.108, bf16[1024,4,80]{0,2,1:T(8,128)(2,1)S(1)} %bitcast.101, bf16[1,1024,4,80]{1,3,2,0:T(8,128)(2,1)S(1)} %bitcast.99), kind=kOutput, calls=%fused_computation.88 | convolution fusion | flops 343933952 | bytes 9383936 | tf_op jit(solution)/shard_map/sub | solution.py:361
  77.0 5.0 %fusion.45 = bf16[4,80,512]{2,1,0:T(8,128)(2,1)S(1)} fusion(bf16[1024,4,80]{0,2,1:T(8,128)(2,1)S(1)} %bitcast.96, f32[4,512,1024]{2,1,0:T(8,128)} %get-tuple-element.36, f32[4,512]{1,0:T(4,128)S(1)} %get-tuple-element.35), kind=kOutput, calls=%fused_computation.51 | convolution fusion | flops 339902464 | bytes 9379840 | tf_op jit(solution)/shard_map/ihqk,ikhe->iqhe/dot_general | solution.py:363
  82.0 0.8 copy-done.8
  82.8 1.7 fusion.44
  84.5 1.1 fusion.41
  85.7 1.7 slice_bitcast_fusion
  87.9 0.6 reshape.565.refs_1_
  88.5 3.8 %convolution_convert_fusion = bf16[1024,1280]{1,0:T(8,128)(2,1)} fusion(bf16[576,1280]{0,1:T(8,128)(2,1)S(1)} %pad_maximum_fusion, bf16[1,1024,576]{1,2,0:T(8,128)(2,1)S(1)} %pad_maximum_fusion.1), kind=kOutput, calls=%fused_computation.27 | convolution fusion | flops 1511260160 | bytes 5275648 | tf_op jit(solution)/shard_map/ijd,de->ije/dot_general | solution.py:379
  92.3 62.3 %reduce_norm_gather.1 = (f32[256,1280]{1,0:T(8,128)}, bf16[4,256,1280]{2,1,0:T(8,128)(2,1)}, bf16[1280,1280]{1,0:T(8,128)(2,1)}) custom-call(bf16[4,256,1280]{2,1,0:T(8,128)(2,1)} %bitcast.114, f32[1,1280]{1,0:T(1,128)} %reshape.565.refs_1_, bf16[160,1280]{1,0:T(8,128)(2,1)} %bitcast.111), custom_call_target="tpu_custom_call" | custom-call | flops 10000000000 | bytes 100000000 | tf_op jit(solution)/shard_map/reduce_norm_gather/pallas_call | solution.py:269
  154.6 12.2 %convolution_convert_fusion.1 = bf16[1024,1280]{1,0:T(8,128)(2,1)} fusion(bf16[1280,1280]{1,0:T(8,128)(2,1)} %get-tuple-element.23, bf16[1024,1280]{1,0:T(8,128)(2,1)} %bitcast.113, bf16[1280,1280]{1,0:T(8,128)(2,1)} %all-gather.2.cloned.1.call-done, f32[1280]{0:T(1024)S(1)} %copy-done.7), kind=kOutput, calls=%fused_computation.28 | convolution fusion | flops 6725304320 | bytes 11801600 | tf_op jit(solution)/shard_map/mf,df->md/dot_general | solution.py:387
  166.8 25.2 %reduce_last.1 = bf16[256,1280]{1,0:T(8,128)(2,1)} custom-call(bf16[4,256,1280]{2,1,0:T(8,128)(2,1)} %bitcast.115, f32[256,1280]{1,0:T(8,128)} %get-tuple-element.24.refs_1_), custom_call_target="tpu_custom_call" | custom-call | flops 10000000000 | bytes 100000000 | tf_op jit(solution)/shard_map/reduce_last/pallas_call | solution.py:269
  192.0 2.0 slice_bitcast_fusion.1
  (33 shorter events, 1.8 us)
Async XLA Ops:
  6.5 6.0 %copy-start.1 = (bf16[320,160]{0,1:T(8,128)(2,1)S(1)}, bf16[320,160]{0,1:T(8,128)(2,1)}, u32[]{:S(2)}) copy-start(bf16[320,160]{0,1:T(8,128)(2,1)} %param.16) | copy-start | bytes 307204
  6.5 148.1 %all-gather.2.cloned.1.call-start = ((), (), s32[]{:S(2)}) async-start(), calls=%async_computation | async-start | bytes 3686400 | tf_op jit(solution)/shard_map/all_gather | solution.py:320
  13.5 42.4 %copy-start = (bf16[1,256,1280]{2,1,0:T(8,128)(2,1)S(1)}, bf16[1,256,1280]{2,1,0:T(8,128)(2,1)}, u32[]{:S(2)}) copy-start(bf16[1,256,1280]{2,1,0:T(8,128)(2,1)} %param.12) | copy-start | bytes 1966084
  61.4 0.7 copy-start.2
  61.4 1.2 copy-start.4
  61.4 2.0 copy-start.5
  61.4 2.0 copy-start.6
  77.0 5.8 %copy-start.8 = (f32[4,512,1024]{2,1,0:T(8,128)S(1)}, f32[4,512,1024]{2,1,0:T(8,128)}, u32[]{:S(2)}) copy-start(f32[4,512,1024]{2,1,0:T(8,128)} %get-tuple-element.34) | copy-start | bytes 25165828
  85.6 2.3 %copy-start.3 = (f32[1280]{0:T(1024)S(1)}, f32[1280]{0:T(1024)}, u32[]{:S(2)}) copy-start(f32[1280]{0:T(1024)} %param.17) | copy-start | bytes 15364
  92.3 62.3 %copy-start.7 = (f32[1280]{0:T(1024)S(1)}, f32[1280]{0:T(1024)}, u32[]{:S(2)}) copy-start(f32[1280]{0:T(1024)} %param.19) | copy-start | bytes 15364
Sparse Core Ops, SparseCore 0:
  56.0 76.5 all-gather.1
